TPU v7x, 32 devices: a whole 2x2x4 slice. The times are simulated.
32 devices in a mesh: data: 2 (over x), inner: 4 (over z), stage: 4 (over y, core).
Axes of the slice: x: 2, y: 2, z: 4, core: 2. Of those that a mesh axis runs over, the one named last changes fastest.
Arguments:
- x_tokens: bfloat16 [32, 256, 768], P(('data', 'stage', 'inner')), parts along dimension 0
- g_cotan: bfloat16 [32, 256, 768], P(('data', 'stage', 'inner')), parts along dimension 0
- w_up: bfloat16 [2, 8, 768, 3072], P(None, ('data', 'stage'), None, 'inner'), parts along dimension 1
- w_down: bfloat16 [2, 8, 3072, 768], P(None, ('data', 'stage'), 'inner'), parts along dimension 1
Outputs:
- output 1: bfloat16 [32, 256, 768], P(('data', 'stage', 'inner')), parts along dimension 0
- output 2: bfloat16 [32, 256, 768], P(('data', 'stage', 'inner')), parts along dimension 0
- output 3: float32 [2, 8, 768, 3072], P(None, ('data', 'stage'), None, 'inner'), parts along dimension 1
- output 4: float32 [2, 8, 3072, 768], P(None, ('data', 'stage'), 'inner'), parts along dimension 1
There are 2 independent parts. A program takes and returns all parts, laid end to end along the dimension named above; each array names one.
All inputs are finite; a program needn't handle non-finite values.
Results may differ from a plain program's by a relative error of at most 0.0161341.
Values are sent between devices in bfloat16 or wider.
A program may use at most 1 GiB of HBM per device.

v0:
```python
import jax
import jax.numpy as jnp
from jax import lax
from jax.sharding import PartitionSpec as P


def gelu_pair(pre_act):
    normal_cdf = 0.5 * (1.0 + lax.erf(pre_act * 0.7071067811865476))
    normal_pdf = jnp.exp(-0.5 * pre_act * pre_act) * 0.3989422804014327
    return pre_act * normal_cdf, normal_cdf + pre_act * normal_pdf


def layer_fwd(h_in, w_one, w_two):
    pre_act = jnp.dot(h_in, w_one, preferred_element_type=jnp.float32)
    act_val = gelu_pair(pre_act)[0].astype(jnp.bfloat16)
    branch = jnp.dot(act_val, w_two, preferred_element_type=jnp.float32)
    return (h_in.astype(jnp.float32) + branch).astype(jnp.bfloat16)


def layer_bwd(h_in, w_one, w_two, g_out):
    pre_act = jnp.dot(h_in, w_one, preferred_element_type=jnp.float32)
    gelu_val, gelu_grad = gelu_pair(pre_act)
    act_val = gelu_val.astype(jnp.bfloat16)
    d_act = lax.dot_general(g_out, w_two, (((1,), (1,)), ((), ())), preferred_element_type=jnp.float32)
    d_pre = (d_act * gelu_grad).astype(jnp.bfloat16)
    grad_one = lax.dot_general(h_in, d_pre, (((0,), (0,)), ((), ())), preferred_element_type=jnp.float32)
    grad_two = lax.dot_general(act_val, g_out, (((0,), (0,)), ((), ())), preferred_element_type=jnp.float32)
    back_term = lax.dot_general(d_pre, w_one, (((1,), (1,)), ((), ())), preferred_element_type=jnp.float32)
    g_in = (g_out.astype(jnp.float32) + back_term).astype(jnp.bfloat16)
    return g_in, grad_one, grad_two


def solution(mesh):
    n_stage = mesh.shape['stage']
    tok_spec = P(('data', 'stage', 'inner'))
    up_spec = P(None, ('data', 'stage'), None, 'inner')
    down_spec = P(None, ('data', 'stage'), 'inner', None)
    fwd_perm = [(src_idx, (src_idx + 1) % n_stage) for src_idx in range(n_stage)]
    bwd_perm = [(src_idx, (src_idx - 1) % n_stage) for src_idx in range(n_stage)]

    def device_step(x_loc, g_loc, w_up, w_down):
        n_virt = w_up.shape[0]
        group_layers = w_up.shape[1]
        d_model = x_loc.shape[2]
        stage_idx = lax.axis_index('stage')
        is_first = stage_idx == 0
        is_last = stage_idx == n_stage - 1
        x_col = lax.all_gather(x_loc, 'stage', axis=0, tiled=True)
        g_col = lax.all_gather(g_loc, 'stage', axis=0, tiled=True)
        n_micro = x_col.shape[0]
        tick_ids = jnp.arange(n_micro + n_stage - 1)
        act_zero = jnp.zeros(x_loc.shape[1:], x_loc.dtype)
        stash_list = []
        act_buf = x_col
        for virt_idx in range(n_virt):
            up_full = lax.all_gather(w_up[virt_idx], 'inner', axis=2, tiled=True)
            down_full = lax.all_gather(w_down[virt_idx], 'inner', axis=1, tiled=True)

            def fwd_tick(loop_state, tick_idx):
                buf_in, recv_act, saved_ins = loop_state
                micro_idx = tick_idx - stage_idx
                is_valid = (micro_idx >= 0) & (micro_idx < n_micro)
                buf_slot = jnp.clip(micro_idx, 0, n_micro - 1)
                from_buf = lax.dynamic_index_in_dim(buf_in, buf_slot, 0, keepdims=False)
                h_act = jnp.where(is_first, from_buf, recv_act)
                layer_ins = []
                for layer_idx in range(group_layers):
                    layer_ins.append(h_act)
                    h_act = layer_fwd(h_act, up_full[layer_idx], down_full[layer_idx])
                old_ins = lax.dynamic_index_in_dim(saved_ins, buf_slot, 0, keepdims=False)
                new_ins = jnp.where(is_valid, jnp.stack(layer_ins), old_ins)
                saved_ins = lax.dynamic_update_index_in_dim(saved_ins, new_ins, buf_slot, 0)
                sent_act = lax.ppermute(h_act, 'stage', fwd_perm)
                done_idx = tick_idx - (n_stage - 1)
                done_slot = jnp.clip(done_idx, 0, n_micro - 1)
                prev_val = lax.dynamic_index_in_dim(buf_in, done_slot, 0, keepdims=False)
                keep_new = is_first & (done_idx >= 0)
                buf_in = lax.dynamic_update_index_in_dim(buf_in, jnp.where(keep_new, sent_act, prev_val), done_slot, 0)
                return (buf_in, sent_act, saved_ins), None

            saved_init = jnp.zeros((n_micro, group_layers) + x_loc.shape[1:], x_loc.dtype)
            end_state = lax.scan(fwd_tick, (act_buf, act_zero, saved_init), tick_ids)[0]
            act_buf = end_state[0]
            stash_list.append(end_state[2])
        y_src = jnp.where(is_first, act_buf, jnp.zeros_like(act_buf))
        y_loc = lax.psum_scatter(y_src, 'stage', scatter_dimension=0, tiled=True)

        grad_buf = g_col
        up_out = [None] * n_virt
        down_out = [None] * n_virt
        for virt_idx in reversed(range(n_virt)):
            up_full = lax.all_gather(w_up[virt_idx], 'inner', axis=2, tiled=True)
            down_full = lax.all_gather(w_down[virt_idx], 'inner', axis=1, tiled=True)
            d_ff = up_full.shape[2]
            saved_ins = stash_list[virt_idx]

            def bwd_tick(loop_state, tick_idx):
                buf_in, recv_grad, acc_one, acc_two = loop_state
                micro_idx = tick_idx - (n_stage - 1 - stage_idx)
                is_valid = (micro_idx >= 0) & (micro_idx < n_micro)
                buf_slot = jnp.clip(micro_idx, 0, n_micro - 1)
                from_buf = lax.dynamic_index_in_dim(buf_in, buf_slot, 0, keepdims=False)
                g_act = jnp.where(is_last, from_buf, recv_grad)
                g_act = jnp.where(is_valid, g_act, jnp.zeros_like(g_act))
                layer_ins = lax.dynamic_index_in_dim(saved_ins, buf_slot, 0, keepdims=False)
                acc_one = list(acc_one)
                acc_two = list(acc_two)
                for layer_idx in reversed(range(group_layers)):
                    g_act, grad_one, grad_two = layer_bwd(layer_ins[layer_idx], up_full[layer_idx], down_full[layer_idx], g_act)
                    acc_one[layer_idx] = acc_one[layer_idx] + grad_one
                    acc_two[layer_idx] = acc_two[layer_idx] + grad_two
                sent_grad = lax.ppermute(g_act, 'stage', bwd_perm)
                done_idx = tick_idx - (n_stage - 1)
                done_slot = jnp.clip(done_idx, 0, n_micro - 1)
                prev_val = lax.dynamic_index_in_dim(buf_in, done_slot, 0, keepdims=False)
                keep_new = is_last & (done_idx >= 0)
                buf_in = lax.dynamic_update_index_in_dim(buf_in, jnp.where(keep_new, sent_grad, prev_val), done_slot, 0)
                return (buf_in, sent_grad, acc_one, acc_two), None

            acc_init_one = [jnp.zeros((d_model, d_ff), jnp.float32) for layer_idx in range(group_layers)]
            acc_init_two = [jnp.zeros((d_ff, d_model), jnp.float32) for layer_idx in range(group_layers)]
            end_state = lax.scan(bwd_tick, (grad_buf, act_zero, acc_init_one, acc_init_two), tick_ids)[0]
            grad_buf = end_state[0]
            up_out[virt_idx] = lax.psum_scatter(jnp.stack(end_state[2]), 'inner', scatter_dimension=2, tiled=True)
            down_out[virt_idx] = lax.psum_scatter(jnp.stack(end_state[3]), 'inner', scatter_dimension=1, tiled=True)
        dx_src = jnp.where(is_last, grad_buf, jnp.zeros_like(grad_buf))
        dx_loc = lax.psum_scatter(dx_src, 'stage', scatter_dimension=0, tiled=True)
        return y_loc, dx_loc, jnp.stack(up_out), jnp.stack(down_out)

    return jax.shard_map(device_step, mesh=mesh, in_specs=(tok_spec, tok_spec, up_spec, down_spec), out_specs=(tok_spec, tok_spec, up_spec, down_spec), check_vma=False)
```

profile of v0, /device:TPU:16, one launch (start us, length us, event | category | flops | bytes accessed | tf_op | source)
XLA Modules:
  0.0 1496.8 jit_solution(390741026547628209)
XLA Ops:
  14.8 15.2 %all-gather.11.cloned.1.call-done = bf16[4,256,768]{2,1,0:T(8,128)(2,1)} async-done(((bf16[1,256,768]{2,1,0:T(8,128)(2,1)}), bf16[4,256,768]{2,1,0:T(8,128)(2,1)}) %all-gather.11.cloned.1.call-update) | async-done | bytes 1572880 | tf_op jit(solution)/shard_map/all_gather | solution.py:48
  30.0 21.0 %all-gather.13.cloned.1.call-done = bf16[4,256,768]{2,1,0:T(8,128)(2,1)} async-done(((bf16[1,256,768]{2,1,0:T(8,128)(2,1)}), bf16[4,256,768]{2,1,0:T(8,128)(2,1)}) %all-gather.13.cloned.1.call-update) | async-done | bytes 1572880 | tf_op jit(solution)/shard_map/all_gather | solution.py:49
  51.0 89.4 %all-gather.15.cloned.1.call-done = bf16[1,1,768,3072]{3,2,1,0:T(8,128)(2,1)} async-done(((bf16[1,1,768,768]{3,2,1,0:T(8,128)(2,1)}), bf16[1,1,768,3072]{3,2,1,0:T(8,128)(2,1)}) %all-gather.15.cloned.1.call-update) | async-done | bytes 4718608 | tf_op jit(solution)/shard_map/all_gather | solution.py:56
  140.5 89.0 %all-gather.17.cloned.1.call-done = bf16[1,1,3072,768]{3,2,1,0:T(8,128)(2,1)} async-done(((bf16[1,1,768,768]{3,2,1,0:T(8,128)(2,1)}), bf16[1,1,3072,768]{3,2,1,0:T(8,128)(2,1)}) %all-gather.17.cloned.1.call-update) | async-done | bytes 4718608 | tf_op jit(solution)/shard_map/all_gather | solution.py:57
  230.7 116.4 %while.70 = (s32[]{:T(128)}, bf16[4,256,768]{2,1,0:T(8,128)(2,1)}, bf16[256,768]{1,0:T(8,128)(2,1)S(1)}, bf16[4,1,256,768]{3,2,1,0:T(8,128)(2,1)}, s32[7]{0:T(12...) while((s32[]{:T(128)}, bf16[4,256,768]{2,1,0:T(8,128)(2,1)}, ...), condition=%wide.region_1.2_spmd, body=%wide.region_0.1_spmd.sunk | while | flops 2421424128 | bytes 30673768 | solution.py:82
  347.1 60.8 %all-gather.21.cloned.1.call-done = bf16[1,1,3072,768]{3,2,1,0:T(8,128)(2,1)} async-done(((bf16[1,1,768,768]{3,2,1,0:T(8,128)(2,1)}), bf16[1,1,3072,768]{3,2,1,0:T(8,128)(2,1)}) %all-gather.21.cloned.1.call-update) | async-done | bytes 4718608 | tf_op jit(solution)/shard_map/all_gather | solution.py:57
  409.2 116.3 %while.71 = (s32[]{:T(128)}, bf16[4,256,768]{2,1,0:T(8,128)(2,1)}, bf16[256,768]{1,0:T(8,128)(2,1)S(1)}, bf16[4,1,256,768]{3,2,1,0:T(8,128)(2,1)}, s32[7]{0:T(12...) while((s32[]{:T(128)}, bf16[4,256,768]{2,1,0:T(8,128)(2,1)}, ...), condition=%wide.region_3.4_spmd, body=%wide.region_2.3_spmd.sunk | while | flops 2421424128 | bytes 30673768 | solution.py:82
  525.6 205.3 %while.72 = (s32[]{:T(128)}, bf16[4,256,768]{2,1,0:T(8,128)(2,1)}, bf16[256,768]{1,0:T(8,128)(2,1)S(1)}, f32[768,3072]{1,0:T(8,128)}, f32[3072,768]{1,0:T(8,128)...) while((s32[]{:T(128)}, bf16[4,256,768]{2,1,0:T(8,128)(2,1)}, ...), condition=%wide.region_6.7_spmd.clone, body=%wide.region_5.6_spmd.clone.sunk | while | flops 6062211072 | bytes 120324592 | solution.py:122
  563.1 7.3 select_add_fusion.9
  570.4 8.9 select_add_fusion.8
  592.5 7.3 select_add_fusion.9
  599.8 8.9 select_add_fusion.8
  622.5 7.3 select_add_fusion.9
  629.7 8.9 select_add_fusion.8
  651.9 7.3 select_add_fusion.9
  659.1 8.9 select_add_fusion.8
  682.8 7.3 select_add_fusion.9
  690.1 8.9 select_add_fusion.8
  712.2 7.3 select_add_fusion.9
  719.5 8.9 select_add_fusion.8
  731.0 208.0 %while.73 = (s32[]{:T(128)}, bf16[4,256,768]{2,1,0:T(8,128)(2,1)}, bf16[256,768]{1,0:T(8,128)(2,1)S(1)}, f32[768,3072]{1,0:T(8,128)}, f32[3072,768]{1,0:T(8,128)...) while((s32[]{:T(128)}, bf16[4,256,768]{2,1,0:T(8,128)(2,1)}, ...), condition=%wide.region_8.9_spmd.clone, body=%wide.region_7.8_spmd.clone.sunk | while | flops 6062211072 | bytes 120324592 | solution.py:122
  775.4 8.9 select_add_fusion.10
  806.6 8.9 select_add_fusion.10
  836.3 8.9 select_add_fusion.10
  866.5 8.9 select_add_fusion.10
  896.3 8.9 select_add_fusion.10
  927.5 8.9 select_add_fusion.10
  943.9 155.9 %reduce-scatter.11.cloned.1.call-done = f32[1,768,768]{2,1,0:T(8,128)} async-done(((f32[1,768,3072]{2,1,0:T(8,128)}), f32[1,768,768]{2,1,0:T(8,128)}) %reduce-scatter.11.cloned.1.call-update) | async-done | bytes 2359312 | tf_op jit(solution)/shard_map/reduce_scatter | solution.py:124
  1104.7 159.2 %reduce-scatter.17.cloned.1.call-done = f32[1,768,768]{2,1,0:T(8,128)} async-done(((f32[1,3072,768]{2,1,0:T(8,128)}), f32[1,768,768]{2,1,0:T(8,128)}) %reduce-scatter.17.cloned.1.call-update) | async-done | bytes 2359312 | tf_op jit(solution)/shard_map/reduce_scatter | solution.py:125
  1263.8 163.9 %reduce-scatter.15.cloned.1.call-done = f32[1,768,768]{2,1,0:T(8,128)} async-done(((f32[1,3072,768]{2,1,0:T(8,128)}), f32[1,768,768]{2,1,0:T(8,128)}) %reduce-scatter.15.cloned.1.call-update) | async-done | bytes 2359312 | tf_op jit(solution)/shard_map/reduce_scatter | solution.py:125
  1432.6 26.6 %reduce-scatter.7.cloned.1.call-done = bf16[1,256,768]{2,1,0:T(8,128)(2,1)} async-done(((bf16[4,256,768]{2,1,0:T(8,128)(2,1)}), bf16[1,256,768]{2,1,0:T(8,128)(2,1)}) %reduce-scatter.7.cloned.1.call-update) | async-done | bytes 393232 | tf_op jit(solution)/shard_map/reduce_scatter | solution.py:86
  1459.1 30.9 %reduce-scatter.9.cloned.1.call-done = bf16[1,256,768]{2,1,0:T(8,128)(2,1)} async-done(((bf16[4,256,768]{2,1,0:T(8,128)(2,1)}), bf16[1,256,768]{2,1,0:T(8,128)(2,1)}) %reduce-scatter.9.cloned.1.call-update) | async-done | bytes 393232 | tf_op jit(solution)/shard_map/reduce_scatter | solution.py:127
  (552 shorter events, 481.0 us)
Async XLA Ops:
  7.2 22.9 %all-gather.11.cloned.1.call-start = ((), (), s32[]{:S(2)}) async-start(), calls=%async_computation.6 | async-start | bytes 1966080 | tf_op jit(solution)/shard_map/all_gather | solution.py:48
  7.9 43.1 %all-gather.13.cloned.1.call-start = ((), (), s32[]{:S(2)}) async-start(), calls=%async_computation.8 | async-start | bytes 1966080 | tf_op jit(solution)/shard_map/all_gather | solution.py:49
  8.7 131.8 %all-gather.15.cloned.1.call-start = ((), (), s32[]{:S(2)}) async-start(), calls=%async_computation.14 | async-start | bytes 5898240 | tf_op jit(solution)/shard_map/all_gather | solution.py:56
  11.9 217.5 %all-gather.17.cloned.1.call-start = ((), (), s32[]{:S(2)}) async-start(), calls=%async_computation.15 | async-start | bytes 5898240 | tf_op jit(solution)/shard_map/all_gather | solution.py:57
  13.5 333.5 %all-gather.19.cloned.1.call-start = ((), (), s32[]{:S(2)}) async-start(), calls=%async_computation.16 | async-start | bytes 5898240 | tf_op jit(solution)/shard_map/all_gather | solution.py:56
  14.1 393.8 %all-gather.21.cloned.1.call-start = ((), (), s32[]{:S(2)}) async-start(), calls=%async_computation.17 | async-start | bytes 5898240 | tf_op jit(solution)/shard_map/all_gather | solution.py:57
  14.7 929.2 %reduce-scatter.13.cloned.1.call-start = ((), (), s32[]{:S(2)}) async-start(), calls=%async_computation.11 | async-start | bytes 11796480 | tf_op jit(solution)/shard_map/reduce_scatter | solution.py:124
  238.8 7.3 collective-permute-start
  255.4 7.3 collective-permute-start
  272.0 7.3 collective-permute-start
  288.7 7.3 collective-permute-start
  321.9 7.3 collective-permute-start
  338.5 7.3 collective-permute-start
  536.4 13.6 collective-permute-start.2
  561.5 19.4 %collective-permute-start.2 = (bf16[256,768]{1,0:T(8,128)(2,1)}, bf16[256,768]{1,0:T(8,128)(2,1)S(1)}, u32[]{:S(2)}, u32[]{:S(2)}) collective-permute-start(bf16[256,768]{1,0:T(8,128)(2,1)} %fusion.156), channel_id=1, source_target_pairs={{0,3},{1,0},{2,1},{3,2},{4,7},{5,4},{6,5},{7,6},{8,11},{9,8},{10,9... | collective-permute-start | bytes 1179656 | tf_op jit(solution)/shard_map/while/body/eval_jaxpr/ppermute | solution.py:112
  592.5 17.8 %collective-permute-start.2 = (bf16[256,768]{1,0:T(8,128)(2,1)}, bf16[256,768]{1,0:T(8,128)(2,1)S(1)}, u32[]{:S(2)}, u32[]{:S(2)}) collective-permute-start(bf16[256,768]{1,0:T(8,128)(2,1)} %fusion.156), channel_id=1, source_target_pairs={{0,3},{1,0},{2,1},{3,2},{4,7},{5,4},{6,5},{7,6},{8,11},{9,8},{10,9... | collective-permute-start | bytes 1179656 | tf_op jit(solution)/shard_map/while/body/eval_jaxpr/ppermute | solution.py:112
  621.8 18.4 %collective-permute-start.2 = (bf16[256,768]{1,0:T(8,128)(2,1)}, bf16[256,768]{1,0:T(8,128)(2,1)S(1)}, u32[]{:S(2)}, u32[]{:S(2)}) collective-permute-start(bf16[256,768]{1,0:T(8,128)(2,1)} %fusion.156), channel_id=1, source_target_pairs={{0,3},{1,0},{2,1},{3,2},{4,7},{5,4},{6,5},{7,6},{8,11},{9,8},{10,9... | collective-permute-start | bytes 1179656 | tf_op jit(solution)/shard_map/while/body/eval_jaxpr/ppermute | solution.py:112
  651.8 17.8 %collective-permute-start.2 = (bf16[256,768]{1,0:T(8,128)(2,1)}, bf16[256,768]{1,0:T(8,128)(2,1)S(1)}, u32[]{:S(2)}, u32[]{:S(2)}) collective-permute-start(bf16[256,768]{1,0:T(8,128)(2,1)} %fusion.156), channel_id=1, source_target_pairs={{0,3},{1,0},{2,1},{3,2},{4,7},{5,4},{6,5},{7,6},{8,11},{9,8},{10,9... | collective-permute-start | bytes 1179656 | tf_op jit(solution)/shard_map/while/body/eval_jaxpr/ppermute | solution.py:112
  681.2 19.4 %collective-permute-start.2 = (bf16[256,768]{1,0:T(8,128)(2,1)}, bf16[256,768]{1,0:T(8,128)(2,1)S(1)}, u32[]{:S(2)}, u32[]{:S(2)}) collective-permute-start(bf16[256,768]{1,0:T(8,128)(2,1)} %fusion.156), channel_id=1, source_target_pairs={{0,3},{1,0},{2,1},{3,2},{4,7},{5,4},{6,5},{7,6},{8,11},{9,8},{10,9... | collective-permute-start | bytes 1179656 | tf_op jit(solution)/shard_map/while/body/eval_jaxpr/ppermute | solution.py:112
  712.1 17.8 %collective-permute-start.2 = (bf16[256,768]{1,0:T(8,128)(2,1)}, bf16[256,768]{1,0:T(8,128)(2,1)S(1)}, u32[]{:S(2)}, u32[]{:S(2)}) collective-permute-start(bf16[256,768]{1,0:T(8,128)(2,1)} %fusion.156), channel_id=1, source_target_pairs={{0,3},{1,0},{2,1},{3,2},{4,7},{5,4},{6,5},{7,6},{8,11},{9,8},{10,9... | collective-permute-start | bytes 1179656 | tf_op jit(solution)/shard_map/while/body/eval_jaxpr/ppermute | solution.py:112
  730.9 368.9 %reduce-scatter.11.cloned.1.call-start = ((), (), s32[]{:S(2)}) async-start(), calls=%async_computation.10 | async-start | bytes 11796480 | tf_op jit(solution)/shard_map/reduce_scatter | solution.py:124
  742.1 14.2 collective-permute-start.3
  768.1 18.0 %collective-permute-start.3 = (bf16[256,768]{1,0:T(8,128)(2,1)}, bf16[256,768]{1,0:T(8,128)(2,1)S(1)}, u32[]{:S(2)}, u32[]{:S(2)}) collective-permute-start(bf16[256,768]{1,0:T(8,128)(2,1)} %fusion.169), channel_id=1, source_target_pairs={{0,3},{1,0},{2,1},{3,2},{4,7},{5,4},{6,5},{7,6},{8,11},{9,8},{10,9... | collective-permute-start | bytes 1179656 | tf_op jit(solution)/shard_map/while/body/eval_jaxpr/ppermute | solution.py:112
  797.8 19.4 %collective-permute-start.3 = (bf16[256,768]{1,0:T(8,128)(2,1)}, bf16[256,768]{1,0:T(8,128)(2,1)S(1)}, u32[]{:S(2)}, u32[]{:S(2)}) collective-permute-start(bf16[256,768]{1,0:T(8,128)(2,1)} %fusion.169), channel_id=1, source_target_pairs={{0,3},{1,0},{2,1},{3,2},{4,7},{5,4},{6,5},{7,6},{8,11},{9,8},{10,9... | collective-permute-start | bytes 1179656 | tf_op jit(solution)/shard_map/while/body/eval_jaxpr/ppermute | solution.py:112
  829.0 18.0 %collective-permute-start.3 = (bf16[256,768]{1,0:T(8,128)(2,1)}, bf16[256,768]{1,0:T(8,128)(2,1)S(1)}, u32[]{:S(2)}, u32[]{:S(2)}) collective-permute-start(bf16[256,768]{1,0:T(8,128)(2,1)} %fusion.169), channel_id=1, source_target_pairs={{0,3},{1,0},{2,1},{3,2},{4,7},{5,4},{6,5},{7,6},{8,11},{9,8},{10,9... | collective-permute-start | bytes 1179656 | tf_op jit(solution)/shard_map/while/body/eval_jaxpr/ppermute | solution.py:112
  858.7 18.5 %collective-permute-start.3 = (bf16[256,768]{1,0:T(8,128)(2,1)}, bf16[256,768]{1,0:T(8,128)(2,1)S(1)}, u32[]{:S(2)}, u32[]{:S(2)}) collective-permute-start(bf16[256,768]{1,0:T(8,128)(2,1)} %fusion.169), channel_id=1, source_target_pairs={{0,3},{1,0},{2,1},{3,2},{4,7},{5,4},{6,5},{7,6},{8,11},{9,8},{10,9... | collective-permute-start | bytes 1179656 | tf_op jit(solution)/shard_map/while/body/eval_jaxpr/ppermute | solution.py:112
  888.9 18.0 %collective-permute-start.3 = (bf16[256,768]{1,0:T(8,128)(2,1)}, bf16[256,768]{1,0:T(8,128)(2,1)S(1)}, u32[]{:S(2)}, u32[]{:S(2)}) collective-permute-start(bf16[256,768]{1,0:T(8,128)(2,1)} %fusion.169), channel_id=1, source_target_pairs={{0,3},{1,0},{2,1},{3,2},{4,7},{5,4},{6,5},{7,6},{8,11},{9,8},{10,9... | collective-permute-start | bytes 1179656 | tf_op jit(solution)/shard_map/while/body/eval_jaxpr/ppermute | solution.py:112
  918.7 19.5 %collective-permute-start.3 = (bf16[256,768]{1,0:T(8,128)(2,1)}, bf16[256,768]{1,0:T(8,128)(2,1)S(1)}, u32[]{:S(2)}, u32[]{:S(2)}) collective-permute-start(bf16[256,768]{1,0:T(8,128)(2,1)} %fusion.169), channel_id=1, source_target_pairs={{0,3},{1,0},{2,1},{3,2},{4,7},{5,4},{6,5},{7,6},{8,11},{9,8},{10,9... | collective-permute-start | bytes 1179656 | tf_op jit(solution)/shard_map/while/body/eval_jaxpr/ppermute | solution.py:112
  939.1 324.8 %reduce-scatter.17.cloned.1.call-start = ((), (), s32[]{:S(2)}) async-start(), calls=%async_computation.13 | async-start | bytes 11796480 | tf_op jit(solution)/shard_map/reduce_scatter | solution.py:125
  939.8 487.9 %reduce-scatter.15.cloned.1.call-start = ((), (), s32[]{:S(2)}) async-start(), calls=%async_computation.12 | async-start | bytes 11796480 | tf_op jit(solution)/shard_map/reduce_scatter | solution.py:125
  940.4 518.7 %reduce-scatter.7.cloned.1.call-start = ((), (), s32[]{:S(2)}) async-start(), calls=%async_computation.7 | async-start | bytes 1966080 | tf_op jit(solution)/shard_map/reduce_scatter | solution.py:86
  942.6 547.4 %reduce-scatter.9.cloned.1.call-start = ((), (), s32[]{:S(2)}) async-start(), calls=%async_computation.9 | async-start | bytes 1966080 | tf_op jit(solution)/shard_map/reduce_scatter | solution.py:127
  (123 other events, 508.7 us)
Sparse Core Ops, SparseCore 0:
  9.5 20.4 all-gather.10
  31.6 19.4 all-gather.12
  53.2 87.2 all-gather.14
  141.9 87.5 all-gather.16
  231.4 87.5 all-gather.18
  320.4 87.5 all-gather.20
  731.0 160.6 reduce-scatter.12
  939.2 160.5 reduce-scatter.10
  1102.2 161.6 reduce-scatter.16
  1266.0 161.6 reduce-scatter.14
  1430.8 28.2 reduce-scatter.6
  1462.1 27.8 reduce-scatter.8
where the time goes:
time: 1500 us
  waiting for transfers between devices  879 us (59%)
  matrix products  428 us (29%)
  local copies, waits for them, and re-layouts  71.3 us (5%)
  other arithmetic  55.1 us (4%)
  loops' own time  38.9 us (3%)
    reduce_scatter x2, waiting for transfers between devices, device_step(): lax.psum_scatter(jnp.stack(end_state[3]), 'inner', scatter_dimension=1, t...  323 us
    reduce_scatter x2, waiting for transfers between devices, device_step(): lax.psum_scatter(jnp.stack(end_state[2]), 'inner', scatter_dimension=2, t...  156 us
    all_gather x2, waiting for transfers between devices, device_step(): down_full = lax.all_gather(w_down[virt_idx], 'inner', axis=1, tiled=True)  150 us
    dot_general x14, matrix products, layer_bwd(): lax.dot_general(h_in, d_pre, (((0,), (0,)), ((), ())), preferred_element_...  119 us
    dot_general x14, matrix products, layer_bwd(): lax.dot_general(act_val, g_out, (((0,), (0,)), ((), ())), preferred_eleme...  98.6 us
    dot_general x14, matrix products, layer_fwd(): branch = jnp.dot(act_val, w_two, preferred_element_type=jnp.float32)  95.3 us
    all_gather x2, waiting for transfers between devices, device_step(): up_full = lax.all_gather(w_up[virt_idx], 'inner', axis=2, tiled=True)  89.4 us
    ppermute x14, waiting for transfers between devices, fwd_tick(): sent_act = lax.ppermute(h_act, 'stage', fwd_perm)  63.7 us
  transfers between devices with their start and end apart: 40, of which 24 were waited for; matrix products, arithmetic and copies ran while one was open for 27% of the time, Pallas kernels for 0%

commit v1 on v0

v1 whole, which is shorter than its diff:
```python
import functools

import jax
import jax.numpy as jnp
from jax import lax
from jax.experimental import pallas as pl
from jax.experimental.pallas import tpu as pltpu
from jax.sharding import PartitionSpec as P

MESH = pl.DeviceIdType.MESH
F32 = jnp.float32
BF16 = jnp.bfloat16
N_CHIP = 8
N_BLK = 4


def gelu_only(z):
    return z * (0.5 * (1.0 + lax.erf(z * 0.7071067811865476)))


def gelu_pair(z):
    cdf = 0.5 * (1.0 + lax.erf(z * 0.7071067811865476))
    pdf = jnp.exp(-0.5 * z * z) * 0.3989422804014327
    return z * cdf, cdf + z * pdf


def dot_nn(a, b):
    return lax.dot_general(a, b, (((1,), (0,)), ((), ())), preferred_element_type=F32)


def dot_nt(a, b):
    return lax.dot_general(a, b, (((1,), (1,)), ((), ())), preferred_element_type=F32)


def dot_tn(a, b):
    return lax.dot_general(a, b, (((0,), (0,)), ((), ())), preferred_element_type=F32)


def chip_z(layer):
    return lax.rem(1 + (layer + 1) // 2, 4)


def chip_y(layer):
    return lax.rem(layer // 2, 2)


def kernel(x_ref, g_ref, wu_ref, wd_ref, y_ref, dx_ref, dwu_ref, dwd_ref,
           w_all, acc, pbuf, hbuf, hout, gbuf, gout, a_s, dz_s,
           x_send, g_send, w_send, w_recv, w_fwd, h_recv, g_recv, h_send, g_sent,
           y_recv, dx_recv, p_send, p_recv, dw_send, dw_recv):
    z = lax.axis_index("inner")
    s = lax.axis_index("stage")
    y = s // 2
    core = lax.rem(s, 2)
    par, half = lax.rem(z, 2), z // 2
    layer = (1 - y) * (5 - 5 * par - 4 * half + 8 * par * half) + y * (6 + par - 4 * half)
    n_chunk, rows, d = hbuf.shape
    partner = 2 * y + (1 - core)
    here = {"inner": z, "stage": s}

    def copy(src, dst, send, recv, dz, ds):
        return pltpu.make_async_remote_copy(
            src_ref=src, dst_ref=dst, send_sem=send, recv_sem=recv,
            device_id={"inner": dz, "stage": ds}, device_id_type=MESH)

    def arrived(slot, sem):
        copy(slot, slot, sem, sem, z, s).wait_recv()

    def sent(slot, sem):
        copy(slot, slot, sem, sem, z, s).wait_send()

    def push(src, dst, send, recv, dz, ds):
        same = (dz == z) & (ds == s)

        @pl.when(same)
        def _():
            pltpu.make_async_copy(src, dst, recv).start()

        @pl.when(jnp.logical_not(same))
        def _():
            copy(src, dst, send, recv, dz, ds).start()

    def pushed(src, send, dz, ds):
        @pl.when(jnp.logical_not((dz == z) & (ds == s)))
        def _():
            sent(src, send)

    def send_weights(v):
        tgt = chip_z(4 * v + s)
        push(wu_ref.at[v], w_all.at[0, z], w_send.at[v, 0], w_recv.at[0, z], tgt, 2 * y)
        push(wd_ref.at[v], w_all.at[1, z], w_send.at[v, 1], w_recv.at[1, z], tgt, 2 * y + 1)

    def weights_sent(v):
        tgt = chip_z(4 * v + s)
        pushed(wu_ref.at[v], w_send.at[v, 0], tgt, 2 * y)
        pushed(wd_ref.at[v], w_send.at[v, 1], tgt, 2 * y + 1)

    chip = 4 * y + z
    send_weights(0)
    for q in range(2):
        slot = 2 * chip + q
        push(x_ref.at[q], hbuf.at[slot], x_send.at[q], h_recv.at[slot], 1, core)
    for k in range(2):
        for b in range(N_BLK):
            acc[k, b] = jnp.zeros(acc.shape[2:], F32)
    weights_sent(0)
    send_weights(1)
    for q in range(2):
        slot = 2 * chip + q
        push(g_ref.at[q], gbuf.at[slot], g_send.at[q], g_recv.at[slot], 1, 2 + core)
    for b in range(N_BLK):
        arrived(w_all.at[core, b], w_recv.at[core, b])
        copy(w_all.at[core, b], w_all.at[core, b], w_fwd.at[b], w_recv.at[core, b], z, partner).start()
    for b in range(N_BLK):
        arrived(w_all.at[1 - core, b], w_recv.at[1 - core, b])

    nxt, prv = layer + 1, layer - 1
    last, first = layer == 7, layer == 0

    def forward(m, carry):
        arrived(hbuf.at[m], h_recv.at[m])
        h = hbuf[m]
        out = h.astype(F32)
        branch = jnp.zeros((rows, d), F32)
        for b in range(N_BLK):
            a = gelu_only(dot_nn(h, w_all[0, b])).astype(BF16)
            branch = branch + dot_nn(a, w_all[1, b])
        hout[m] = (out + branch).astype(BF16)

        @pl.when(layer < 7)
        def _():
            copy(hout.at[m], hbuf.at[m], h_send.at[m], h_recv.at[m],
                 chip_z(nxt), 2 * chip_y(nxt) + core).start()

        @pl.when(last)
        def _():
            home, q = m // 2, lax.rem(m, 2)
            push(hout.at[m], y_ref.at[q], h_send.at[m], y_recv.at[q],
                 lax.rem(home, 4), 2 * (home // 4) + core)
        return carry

    lax.fori_loop(0, n_chunk, forward, 0)

    def backward(p, carry):
        for q in range(2):
            m = 2 * p + q
            arrived(gbuf.at[m], g_recv.at[m])
            h = hbuf[m]
            g = gbuf[m]
            back = jnp.zeros((rows, d), F32)
            for b in range(N_BLK):
                act, grad = gelu_pair(dot_nn(h, w_all[0, b]))
                dz = (dot_nt(g, w_all[1, b]) * grad).astype(BF16)
                a_s[b, pl.ds(q * rows, rows), :] = act.astype(BF16)
                dz_s[b, pl.ds(q * rows, rows), :] = dz
                back = back + dot_nt(dz, w_all[0, b])
            gout[m] = (g.astype(F32) + back).astype(BF16)

            @pl.when(layer > 0)
            def _():
                copy(gout.at[m], gbuf.at[m], g_sent.at[m], g_recv.at[m],
                     chip_z(prv), 2 * chip_y(prv) + core).start()

            @pl.when(first)
            def _():
                push(gout.at[m], dx_ref.at[q], g_sent.at[m], dx_recv.at[q],
                     lax.rem(p, 4), 2 * (p // 4) + core)

        h2 = hbuf[pl.ds(2 * p, 2)].reshape(2 * rows, d)
        g2 = gbuf[pl.ds(2 * p, 2)].reshape(2 * rows, d)
        for b in range(N_BLK):
            acc[0, b] += dot_tn(h2, dz_s[b])
            acc[1, b] += dot_tn(a_s[b], g2)
        return carry

    lax.fori_loop(0, n_chunk // 2, backward, 0)

    for b in range(N_BLK):
        copy(acc.at[1 - core, b], pbuf.at[b], p_send.at[b], p_recv.at[b], z, partner).start()
    virt = layer // 4
    owner = lax.rem(layer, 4)
    for b in range(N_BLK):
        arrived(pbuf.at[b], p_recv.at[b])
        acc[core, b] += pbuf[b]

        @pl.when(core == 0)
        def _():
            push(acc.at[0, b], dwu_ref.at[virt], dw_send.at[b], dw_recv.at[0, virt], b, owner)

        @pl.when(core == 1)
        def _():
            push(acc.at[1, b], dwd_ref.at[virt], dw_send.at[b], dw_recv.at[1, virt], b, owner)

    for q in range(2):
        pushed(x_ref.at[q], x_send.at[q], 1, core)
        pushed(g_ref.at[q], g_send.at[q], 1, 2 + core)
        arrived(y_ref.at[q], y_recv.at[q])
        arrived(dx_ref.at[q], dx_recv.at[q])
    weights_sent(1)

    def drain(m, carry):
        home = m // 2
        mine = home == chip

        @pl.when(jnp.logical_not(last & mine))
        def _():
            sent(hout.at[m], h_send.at[m])

        @pl.when(jnp.logical_not(first & mine))
        def _():
            sent(gout.at[m], g_sent.at[m])
        return carry

    lax.fori_loop(0, n_chunk, drain, 0)
    for b in range(N_BLK):
        sent(w_all.at[core, b], w_fwd.at[b])
        sent(acc.at[1 - core, b], p_send.at[b])
        pushed(acc.at[core, b], dw_send.at[b], b, owner)
    for v in range(2):
        arrived(dwu_ref.at[v], dw_recv.at[0, v])
        arrived(dwd_ref.at[v], dw_recv.at[1, v])


def solution(mesh):
    tok_spec = P(('data', 'stage', 'inner'))
    up_spec = P(None, ('data', 'stage'), None, 'inner')
    down_spec = P(None, ('data', 'stage'), 'inner', None)

    def device_step(x_loc, g_loc, w_up, w_down):
        _, tokens, d = x_loc.shape
        ff = w_up.shape[3]
        rows = tokens // 2
        n_chunk = 2 * N_CHIP
        dma = pltpu.SemaphoreType.DMA
        hbm = pl.BlockSpec(memory_space=pl.ANY)
        flops = 7 * 2 * d * ff * N_BLK * n_chunk * rows
        y, dx, dwu, dwd = pl.pallas_call(
            kernel,
            out_shape=(
                jax.ShapeDtypeStruct((2, rows, d), BF16),
                jax.ShapeDtypeStruct((2, rows, d), BF16),
                jax.ShapeDtypeStruct((2, d, ff), F32),
                jax.ShapeDtypeStruct((2, ff, d), F32),
            ),
            in_specs=[hbm] * 4,
            out_specs=(hbm,) * 4,
            scratch_shapes=[
                pltpu.VMEM((2, N_BLK, d, ff), BF16),
                pltpu.VMEM((2, N_BLK, d, ff), F32),
                pltpu.VMEM((N_BLK, d, ff), F32),
                pltpu.VMEM((n_chunk, rows, d), BF16),
                pltpu.VMEM((n_chunk, rows, d), BF16),
                pltpu.VMEM((n_chunk, rows, d), BF16),
                pltpu.VMEM((n_chunk, rows, d), BF16),
                pltpu.VMEM((N_BLK, 2 * rows, ff), BF16),
                pltpu.VMEM((N_BLK, 2 * rows, ff), BF16),
                dma((2,)), dma((2,)), dma((2, 2)), dma((2, N_BLK)), dma((N_BLK,)),
                dma((n_chunk,)), dma((n_chunk,)), dma((n_chunk,)), dma((n_chunk,)),
                dma((2,)), dma((2,)), dma((N_BLK,)), dma((N_BLK,)), dma((N_BLK,)), dma((2, 2)),
            ],
            compiler_params=pltpu.CompilerParams(
                has_side_effects=True, vmem_limit_bytes=66 * 1000 * 1000),
            cost_estimate=pl.CostEstimate(flops=flops, bytes_accessed=40_000_000, transcendentals=0),
        )(x_loc.reshape(2, rows, d), g_loc.reshape(2, rows, d),
          w_up.reshape(2, d, ff), w_down.reshape(2, ff, d))
        return (y.reshape(x_loc.shape), dx.reshape(x_loc.shape),
                dwu.reshape(w_up.shape), dwd.reshape(w_down.shape))

    return jax.shard_map(device_step, mesh=mesh, in_specs=(tok_spec, tok_spec, up_spec, down_spec),
                         out_specs=(tok_spec, tok_spec, up_spec, down_spec), check_vma=False)
```

time: 1500 us -> 635 us (0.42)
  the two profiles are of different devices: /device:TPU:16 before, /device:TPU:24 now
where the time goes in v1:
time: 635 us
  Pallas kernels  623 us (98%)
  local copies, waits for them, and re-layouts  10.8 us (2%)
    pallas_call x1, Pallas kernels, device_step(): pl.pallas_call(kernel, out_shape=(jax.ShapeDtypeStruct((2, rows, d), BF16...  623 us

profile of v1, /device:TPU:24, one launch (start us, length us, event | category | flops | bytes accessed | tf_op | source)
XLA Modules:
  0.0 634.8 jit_solution(15697962753315381133)
XLA Ops:
  0.6 623.4 %shard_map.75 = (bf16[2,128,768]{2,1,0:T(8,128)(2,1)}, bf16[2,128,768]{2,1,0:T(8,128)(2,1)}, f32[2,768,768]{2,1,0:T(8,128)}, f32[2,768,768]{2,1,0:T(8,128)}) custom-call(bf16[2,128,768]{2,1,0:T(8,128)(2,1)} %bitcast.20, bf16[2,128,768]{2,1,0:T(8,128)(2,1)} %bitcast.21, bf16[2,768,768]{2,1,0:T(8,128)(2,1)} %bitcast.18, bf16[2,768,768]{2,1,0:T(8,128)(2,1)} %bitcast.19), custom_call_target="tpu_custom_call" | custom-call | flops 67645734912 | bytes 40000000 | tf_op jit(solution)/shard_map/pallas_call | solution.py:237
  624.1 1.8 copy.14
  625.8 0.0 slice-start
  625.8 1.9 copy.15
  627.8 0.0 slice-start.1
  627.8 4.9 copy.16
  632.6 0.0 slice-done
  632.6 0.0 slice-done.1
  632.7 2.2 copy.17
  (1 shorter events, 0.0 us)
Async XLA Ops:
  625.8 6.8 %slice-start = ((s8[4718592]{0:T(1024)(128)(4,1)}), s8[4194304]{0:T(1024)(128)(4,1)S(1)}, s32[]{:S(2)}) async-start(s8[4718592]{0:T(1024)(128)(4,1)} %bitcast.12), calls=%async_computation | async-start | bytes 8388608
  627.8 4.9 slice-start.1

commit v2 on v1

--- a/solution.py
+++ b/solution.py
@@ -103,8 +103,13 @@
     for k in range(2):
         for b in range(N_BLK):
             acc[k, b] = jnp.zeros(acc.shape[2:], F32)
-    weights_sent(0)
-    send_weights(1)
+    early = layer < 4
+
+    @pl.when(jnp.logical_not(early))
+    def _():
+        weights_sent(0)
+        send_weights(1)
+
     for q in range(2):
         slot = 2 * chip + q
         push(g_ref.at[q], gbuf.at[slot], g_send.at[q], g_recv.at[slot], 1, 2 + core)
@@ -114,10 +119,15 @@
     for b in range(N_BLK):
         arrived(w_all.at[1 - core, b], w_recv.at[1 - core, b])
 
+    @pl.when(early)
+    def _():
+        weights_sent(0)
+        send_weights(1)
+
     nxt, prv = layer + 1, layer - 1
-    last, first = layer == 7, layer == 0
-
-    def forward(m, carry):
+    last, first = layer == N_CHIP - 1, layer == 0
+
+    def forward(m):
         arrived(hbuf.at[m], h_recv.at[m])
         h = hbuf[m]
         out = h.astype(F32)
@@ -127,7 +137,7 @@
             branch = branch + dot_nn(a, w_all[1, b])
         hout[m] = (out + branch).astype(BF16)
 
-        @pl.when(layer < 7)
+        @pl.when(jnp.logical_not(last))
         def _():
             copy(hout.at[m], hbuf.at[m], h_send.at[m], h_recv.at[m],
                  chip_z(nxt), 2 * chip_y(nxt) + core).start()
@@ -137,59 +147,76 @@
             home, q = m // 2, lax.rem(m, 2)
             push(hout.at[m], y_ref.at[q], h_send.at[m], y_recv.at[q],
                  lax.rem(home, 4), 2 * (home // 4) + core)
-        return carry
-
-    lax.fori_loop(0, n_chunk, forward, 0)
-
-    def backward(p, carry):
-        for q in range(2):
-            m = 2 * p + q
-            arrived(gbuf.at[m], g_recv.at[m])
-            h = hbuf[m]
-            g = gbuf[m]
-            back = jnp.zeros((rows, d), F32)
-            for b in range(N_BLK):
-                act, grad = gelu_pair(dot_nn(h, w_all[0, b]))
-                dz = (dot_nt(g, w_all[1, b]) * grad).astype(BF16)
-                a_s[b, pl.ds(q * rows, rows), :] = act.astype(BF16)
-                dz_s[b, pl.ds(q * rows, rows), :] = dz
-                back = back + dot_nt(dz, w_all[0, b])
-            gout[m] = (g.astype(F32) + back).astype(BF16)
-
-            @pl.when(layer > 0)
-            def _():
-                copy(gout.at[m], gbuf.at[m], g_sent.at[m], g_recv.at[m],
-                     chip_z(prv), 2 * chip_y(prv) + core).start()
-
-            @pl.when(first)
-            def _():
-                push(gout.at[m], dx_ref.at[q], g_sent.at[m], dx_recv.at[q],
-                     lax.rem(p, 4), 2 * (p // 4) + core)
-
+
+    def backward(m):
+        q = lax.rem(m, 2)
+        arrived(gbuf.at[m], g_recv.at[m])
+        h = hbuf[m]
+        g = gbuf[m]
+        back = jnp.zeros((rows, d), F32)
+        for b in range(N_BLK):
+            act, grad = gelu_pair(dot_nn(h, w_all[0, b]))
+            dz = (dot_nt(g, w_all[1, b]) * grad).astype(BF16)
+            a_s[b, q] = act.astype(BF16)
+            dz_s[b, q] = dz
+            back = back + dot_nt(dz, w_all[0, b])
+        gout[m] = (g.astype(F32) + back).astype(BF16)
+
+        @pl.when(jnp.logical_not(first))
+        def _():
+            copy(gout.at[m], gbuf.at[m], g_sent.at[m], g_recv.at[m],
+                 chip_z(prv), 2 * chip_y(prv) + core).start()
+
+        @pl.when(first)
+        def _():
+            home = m // 2
+            push(gout.at[m], dx_ref.at[q], g_sent.at[m], dx_recv.at[q],
+                 lax.rem(home, 4), 2 * (home // 4) + core)
+
+    def weight_grads(p):
         h2 = hbuf[pl.ds(2 * p, 2)].reshape(2 * rows, d)
         g2 = gbuf[pl.ds(2 * p, 2)].reshape(2 * rows, d)
         for b in range(N_BLK):
-            acc[0, b] += dot_tn(h2, dz_s[b])
-            acc[1, b] += dot_tn(a_s[b], g2)
+            acc[0, b] += dot_tn(h2, dz_s[b].reshape(2 * rows, -1))
+            acc[1, b] += dot_tn(a_s[b].reshape(2 * rows, -1), g2)
+
+    turn = 4 * (N_CHIP - 1) + 1
+
+    def tick(t, carry):
+        m_f = t - 2 * layer
+        m_b = t - turn + 2 * layer
+
+        @pl.when((m_f >= 0) & (m_f < n_chunk))
+        def _():
+            forward(m_f)
+
+        @pl.when((m_b >= 0) & (m_b < n_chunk))
+        def _():
+            backward(m_b)
+
+            @pl.when(lax.rem(m_b, 2) == 1)
+            def _():
+                weight_grads(m_b // 2)
         return carry
 
-    lax.fori_loop(0, n_chunk // 2, backward, 0)
-
-    for b in range(N_BLK):
-        copy(acc.at[1 - core, b], pbuf.at[b], p_send.at[b], p_recv.at[b], z, partner).start()
+    lax.fori_loop(0, n_chunk + turn, tick, 0)
+
+    order = [i + (1 - half) * (3 - 2 * i) for i in range(N_BLK)]
+    for i, b in enumerate(order):
+        copy(acc.at[1 - core, b], pbuf.at[i], p_send.at[i], p_recv.at[i], z, partner).start()
     virt = layer // 4
     owner = lax.rem(layer, 4)
-    for b in range(N_BLK):
-        arrived(pbuf.at[b], p_recv.at[b])
-        acc[core, b] += pbuf[b]
+    for i, b in enumerate(order):
+        arrived(pbuf.at[i], p_recv.at[i])
+        acc[core, b] += pbuf[i]
 
         @pl.when(core == 0)
         def _():
-            push(acc.at[0, b], dwu_ref.at[virt], dw_send.at[b], dw_recv.at[0, virt], b, owner)
+            push(acc.at[0, b], dwu_ref.at[virt], dw_send.at[i], dw_recv.at[0, virt], b, owner)
 
         @pl.when(core == 1)
         def _():
-            push(acc.at[1, b], dwd_ref.at[virt], dw_send.at[b], dw_recv.at[1, virt], b, owner)
+            push(acc.at[1, b], dwd_ref.at[virt], dw_send.at[i], dw_recv.at[1, virt], b, owner)
 
     for q in range(2):
         pushed(x_ref.at[q], x_send.at[q], 1, core)
@@ -212,10 +239,10 @@
         return carry
 
     lax.fori_loop(0, n_chunk, drain, 0)
-    for b in range(N_BLK):
-        sent(w_all.at[core, b], w_fwd.at[b])
-        sent(acc.at[1 - core, b], p_send.at[b])
-        pushed(acc.at[core, b], dw_send.at[b], b, owner)
+    for i, b in enumerate(order):
+        sent(w_all.at[core, i], w_fwd.at[i])
+        sent(acc.at[1 - core, b], p_send.at[i])
+        pushed(acc.at[core, b], dw_send.at[i], b, owner)
     for v in range(2):
         arrived(dwu_ref.at[v], dw_recv.at[0, v])
         arrived(dwd_ref.at[v], dw_recv.at[1, v])
@@ -252,8 +279,8 @@
                 pltpu.VMEM((n_chunk, rows, d), BF16),
                 pltpu.VMEM((n_chunk, rows, d), BF16),
                 pltpu.VMEM((n_chunk, rows, d), BF16),
-                pltpu.VMEM((N_BLK, 2 * rows, ff), BF16),
-                pltpu.VMEM((N_BLK, 2 * rows, ff), BF16),
+                pltpu.VMEM((N_BLK, 2, rows, ff), BF16),
+                pltpu.VMEM((N_BLK, 2, rows, ff), BF16),
                 dma((2,)), dma((2,)), dma((2, 2)), dma((2, N_BLK)), dma((N_BLK,)),
                 dma((n_chunk,)), dma((n_chunk,)), dma((n_chunk,)), dma((n_chunk,)),
                 dma((2,)), dma((2,)), dma((N_BLK,)), dma((N_BLK,)), dma((N_BLK,)), dma((2, 2)),

time: 635 us -> 617 us (0.972)
  the two profiles are of different devices: /device:TPU:24 before, /device:TPU:16 now
where the time goes in v2:
time: 617 us
  Pallas kernels  606 us (98%)
  local copies, waits for them, and re-layouts  10.8 us (2%)
    pallas_call x1, Pallas kernels, device_step(): pl.pallas_call(kernel, out_shape=(jax.ShapeDtypeStruct((2, rows, d), BF16...  606 us

profile of v2, /device:TPU:16, one launch (start us, length us, event | category | flops | bytes accessed | tf_op | source)
XLA Modules:
  0.0 617.3 jit_solution(6187543861146561902)
XLA Ops:
  0.6 605.9 %shard_map.75 = (bf16[2,128,768]{2,1,0:T(8,128)(2,1)}, bf16[2,128,768]{2,1,0:T(8,128)(2,1)}, f32[2,768,768]{2,1,0:T(8,128)}, f32[2,768,768]{2,1,0:T(8,128)}) custom-call(bf16[2,128,768]{2,1,0:T(8,128)(2,1)} %bitcast.20, bf16[2,128,768]{2,1,0:T(8,128)(2,1)} %bitcast.21, bf16[2,768,768]{2,1,0:T(8,128)(2,1)} %bitcast.18, bf16[2,768,768]{2,1,0:T(8,128)(2,1)} %bitcast.19), custom_call_target="tpu_custom_call" | custom-call | flops 67645734912 | bytes 40000000 | tf_op jit(solution)/shard_map/pallas_call | solution.py:264
  606.5 1.8 copy.14
  608.3 0.0 slice-start
  608.3 1.9 copy.15
  610.2 0.0 slice-start.1
  610.2 4.9 copy.16
  615.1 0.0 slice-done
  615.1 0.0 slice-done.1
  615.1 2.2 copy.17
  (1 shorter events, 0.0 us)
Async XLA Ops:
  608.3 6.8 %slice-start = ((s8[4718592]{0:T(1024)(128)(4,1)}), s8[4194304]{0:T(1024)(128)(4,1)S(1)}, s32[]{:S(2)}) async-start(s8[4718592]{0:T(1024)(128)(4,1)} %bitcast.12), calls=%async_computation | async-start | bytes 8388608
  610.2 4.9 slice-start.1

commit v3 on v2

--- a/solution.py
+++ b/solution.py
@@ -47,7 +47,7 @@
 def kernel(x_ref, g_ref, wu_ref, wd_ref, y_ref, dx_ref, dwu_ref, dwd_ref,
            w_all, acc, pbuf, hbuf, hout, gbuf, gout, a_s, dz_s,
            x_send, g_send, w_send, w_recv, w_fwd, h_recv, g_recv, h_send, g_sent,
-           y_recv, dx_recv, p_send, p_recv, dw_send, dw_recv):
+           y_recv, dx_recv, p_send, p_recv, dw_send, dw_recv, go):
     z = lax.axis_index("inner")
     s = lax.axis_index("stage")
     y = s // 2
@@ -56,7 +56,6 @@
     layer = (1 - y) * (5 - 5 * par - 4 * half + 8 * par * half) + y * (6 + par - 4 * half)
     n_chunk, rows, d = hbuf.shape
     partner = 2 * y + (1 - core)
-    here = {"inner": z, "stage": s}
 
     def copy(src, dst, send, recv, dz, ds):
         return pltpu.make_async_remote_copy(
@@ -95,7 +94,7 @@
         pushed(wu_ref.at[v], w_send.at[v, 0], tgt, 2 * y)
         pushed(wd_ref.at[v], w_send.at[v, 1], tgt, 2 * y + 1)
 
-    chip = 4 * y + z
+    chip = 4 * half + 2 * y + par
     send_weights(0)
     for q in range(2):
         slot = 2 * chip + q
@@ -103,9 +102,10 @@
     for k in range(2):
         for b in range(N_BLK):
             acc[k, b] = jnp.zeros(acc.shape[2:], F32)
-    early = layer < 4
-
-    @pl.when(jnp.logical_not(early))
+    early = (y == 0) & (layer < 4)
+    late = (y == 0) & (layer >= 4)
+
+    @pl.when(y == 1)
     def _():
         weights_sent(0)
         send_weights(1)
@@ -113,6 +113,12 @@
     for q in range(2):
         slot = 2 * chip + q
         push(g_ref.at[q], gbuf.at[slot], g_send.at[q], g_recv.at[slot], 1, 2 + core)
+    @pl.when(late)
+    def _():
+        weights_sent(0)
+        pl.semaphore_wait(go, 1)
+        send_weights(1)
+
     for b in range(N_BLK):
         arrived(w_all.at[core, b], w_recv.at[core, b])
         copy(w_all.at[core, b], w_all.at[core, b], w_fwd.at[b], w_recv.at[core, b], z, partner).start()
@@ -121,6 +127,8 @@
 
     @pl.when(early)
     def _():
+        pl.semaphore_signal(go, inc=1, device_id={"inner": lax.rem(z + 2, 4), "stage": s},
+                            device_id_type=MESH)
         weights_sent(0)
         send_weights(1)
 
@@ -146,7 +154,7 @@
         def _():
             home, q = m // 2, lax.rem(m, 2)
             push(hout.at[m], y_ref.at[q], h_send.at[m], y_recv.at[q],
-                 lax.rem(home, 4), 2 * (home // 4) + core)
+                 2 * (home // 4) + lax.rem(home, 2), 2 * lax.rem(home // 2, 2) + core)
 
     def backward(m):
         q = lax.rem(m, 2)
@@ -171,7 +179,7 @@
         def _():
             home = m // 2
             push(gout.at[m], dx_ref.at[q], g_sent.at[m], dx_recv.at[q],
-                 lax.rem(home, 4), 2 * (home // 4) + core)
+                 2 * (home // 4) + lax.rem(home, 2), 2 * lax.rem(home // 2, 2) + core)
 
     def weight_grads(p):
         h2 = hbuf[pl.ds(2 * p, 2)].reshape(2 * rows, d)
@@ -284,6 +292,7 @@
                 dma((2,)), dma((2,)), dma((2, 2)), dma((2, N_BLK)), dma((N_BLK,)),
                 dma((n_chunk,)), dma((n_chunk,)), dma((n_chunk,)), dma((n_chunk,)),
                 dma((2,)), dma((2,)), dma((N_BLK,)), dma((N_BLK,)), dma((N_BLK,)), dma((2, 2)),
+                pltpu.SemaphoreType.REGULAR,
             ],
             compiler_params=pltpu.CompilerParams(
                 has_side_effects=True, vmem_limit_bytes=66 * 1000 * 1000),

time: 617 us -> 598 us (0.969)
  Pallas kernels: 606 us -> 585 us
    pallas_call x1, Pallas kernels: 606 us -> 585 us  [device_step(): pl.pallas_call(kernel, out_shape=(jax.ShapeDtypeStruct((2, rows, d), BF16...]
where the time goes in v3:
time: 598 us; the launch traced here: 596 us
  Pallas kernels  585 us (98%)
  local copies, waits for them, and re-layouts  10.8 us (2%)
    pallas_call x1, Pallas kernels, device_step(): pl.pallas_call(kernel, out_shape=(jax.ShapeDtypeStruct((2, rows, d), BF16...  585 us

profile of v3, /device:TPU:16, one launch (start us, length us, event | category | flops | bytes accessed | tf_op | source)
XLA Modules:
  0.0 596.5 jit_solution(3838660455478444024)
XLA Ops:
  0.6 585.1 %shard_map.75 = (bf16[2,128,768]{2,1,0:T(8,128)(2,1)}, bf16[2,128,768]{2,1,0:T(8,128)(2,1)}, f32[2,768,768]{2,1,0:T(8,128)}, f32[2,768,768]{2,1,0:T(8,128)}) custom-call(bf16[2,128,768]{2,1,0:T(8,128)(2,1)} %bitcast.20, bf16[2,128,768]{2,1,0:T(8,128)(2,1)} %bitcast.21, bf16[2,768,768]{2,1,0:T(8,128)(2,1)} %bitcast.18, bf16[2,768,768]{2,1,0:T(8,128)(2,1)} %bitcast.19), custom_call_target="tpu_custom_call" | custom-call | flops 67645734912 | bytes 40000000 | tf_op jit(solution)/shard_map/pallas_call | solution.py:272
  585.7 1.8 copy.14
  587.5 0.0 slice-start
  587.5 1.9 copy.15
  589.4 0.0 slice-start.1
  589.4 4.9 copy.16
  594.3 0.0 slice-done
  594.3 0.0 slice-done.1
  594.3 2.2 copy.17
  (1 shorter events, 0.0 us)
Async XLA Ops:
  587.5 6.8 %slice-start = ((s8[4718592]{0:T(1024)(128)(4,1)}), s8[4194304]{0:T(1024)(128)(4,1)S(1)}, s32[]{:S(2)}) async-start(s8[4718592]{0:T(1024)(128)(4,1)} %bitcast.12), calls=%async_computation | async-start | bytes 8388608
  589.4 4.9 slice-start.1

commit v4 on v2

--- a/solution.py
+++ b/solution.py
@@ -56,7 +56,6 @@
     layer = (1 - y) * (5 - 5 * par - 4 * half + 8 * par * half) + y * (6 + par - 4 * half)
     n_chunk, rows, d = hbuf.shape
     partner = 2 * y + (1 - core)
-    here = {"inner": z, "stage": s}
 
     def copy(src, dst, send, recv, dz, ds):
         return pltpu.make_async_remote_copy(
@@ -95,7 +94,7 @@
         pushed(wu_ref.at[v], w_send.at[v, 0], tgt, 2 * y)
         pushed(wd_ref.at[v], w_send.at[v, 1], tgt, 2 * y + 1)
 
-    chip = 4 * y + z
+    chip = 4 * half + 2 * y + par
     send_weights(0)
     for q in range(2):
         slot = 2 * chip + q
@@ -103,27 +102,18 @@
     for k in range(2):
         for b in range(N_BLK):
             acc[k, b] = jnp.zeros(acc.shape[2:], F32)
-    early = layer < 4
-
-    @pl.when(jnp.logical_not(early))
-    def _():
-        weights_sent(0)
-        send_weights(1)
-
+    weights_sent(0)
+    send_weights(1)
     for q in range(2):
         slot = 2 * chip + q
         push(g_ref.at[q], gbuf.at[slot], g_send.at[q], g_recv.at[slot], 1, 2 + core)
+
     for b in range(N_BLK):
         arrived(w_all.at[core, b], w_recv.at[core, b])
         copy(w_all.at[core, b], w_all.at[core, b], w_fwd.at[b], w_recv.at[core, b], z, partner).start()
     for b in range(N_BLK):
         arrived(w_all.at[1 - core, b], w_recv.at[1 - core, b])
 
-    @pl.when(early)
-    def _():
-        weights_sent(0)
-        send_weights(1)
-
     nxt, prv = layer + 1, layer - 1
     last, first = layer == N_CHIP - 1, layer == 0
 
@@ -146,7 +136,7 @@
         def _():
             home, q = m // 2, lax.rem(m, 2)
             push(hout.at[m], y_ref.at[q], h_send.at[m], y_recv.at[q],
-                 lax.rem(home, 4), 2 * (home // 4) + core)
+                 2 * (home // 4) + lax.rem(home, 2), 2 * lax.rem(home // 2, 2) + core)
 
     def backward(m):
         q = lax.rem(m, 2)
@@ -171,7 +161,7 @@
         def _():
             home = m // 2
             push(gout.at[m], dx_ref.at[q], g_sent.at[m], dx_recv.at[q],
-                 lax.rem(home, 4), 2 * (home // 4) + core)
+                 2 * (home // 4) + lax.rem(home, 2), 2 * lax.rem(home // 2, 2) + core)
 
     def weight_grads(p):
         h2 = hbuf[pl.ds(2 * p, 2)].reshape(2 * rows, d)

time: 617 us -> 576 us (0.934)
  Pallas kernels: 606 us -> 565 us
    pallas_call x1, Pallas kernels: 606 us -> 565 us  [device_step(): pl.pallas_call(kernel, out_shape=(jax.ShapeDtypeStruct((2, rows, d), BF16...]
where the time goes in v4:
time: 576 us
  Pallas kernels  565 us (98%)
  local copies, waits for them, and re-layouts  10.8 us (2%)
    pallas_call x1, Pallas kernels, device_step(): pl.pallas_call(kernel, out_shape=(jax.ShapeDtypeStruct((2, rows, d), BF16...  565 us

profile of v4, /device:TPU:16, one launch (start us, length us, event | category | flops | bytes accessed | tf_op | source)
XLA Modules:
  0.0 576.0 jit_solution(14972787526436638126)
XLA Ops:
  0.6 564.6 %shard_map.75 = (bf16[2,128,768]{2,1,0:T(8,128)(2,1)}, bf16[2,128,768]{2,1,0:T(8,128)(2,1)}, f32[2,768,768]{2,1,0:T(8,128)}, f32[2,768,768]{2,1,0:T(8,128)}) custom-call(bf16[2,128,768]{2,1,0:T(8,128)(2,1)} %bitcast.20, bf16[2,128,768]{2,1,0:T(8,128)(2,1)} %bitcast.21, bf16[2,768,768]{2,1,0:T(8,128)(2,1)} %bitcast.18, bf16[2,768,768]{2,1,0:T(8,128)(2,1)} %bitcast.19), custom_call_target="tpu_custom_call" | custom-call | flops 67645734912 | bytes 40000000 | tf_op jit(solution)/shard_map/pallas_call | solution.py:254
  565.2 1.8 copy.14
  567.0 0.0 slice-start
  567.0 1.9 copy.15
  568.9 0.0 slice-start.1
  568.9 4.9 copy.16
  573.8 0.0 slice-done
  573.8 0.0 slice-done.1
  573.8 2.2 copy.17
  (1 shorter events, 0.0 us)
Async XLA Ops:
  567.0 6.8 %slice-start = ((s8[4718592]{0:T(1024)(128)(4,1)}), s8[4194304]{0:T(1024)(128)(4,1)S(1)}, s32[]{:S(2)}) async-start(s8[4718592]{0:T(1024)(128)(4,1)} %bitcast.12), calls=%async_computation | async-start | bytes 8388608
  568.9 4.9 slice-start.1
